TPU v7x, 32 devices: a 4x2x2 block of a 4x4x8 slice. The times are simulated.
32 devices in a mesh: dp: 4 (over y, z), ep: 8 (over x, core).
Axes of the slice: x: 4, y: 2, z: 2, core: 2. Of those that a mesh axis runs over, the one named last changes fastest.
The devices are a block of a 4x4x8 slice.
Arguments:
- x_in: bfloat16 [384, 384, 768], P(('dp', 'ep')), parts along dimension 0
- pad_mask: int32 [384, 384], P(('dp', 'ep')), parts along dimension 0
- rel_bias: float32 [12, 384, 384], replicated
- expert_idx: int32 [2, 384, 384], P(None, ('dp', 'ep')), parts along dimension 1
- norm_scale: float32 [2, 2, 768], replicated
- w_query: bfloat16 [2, 768, 768], replicated
- w_key: bfloat16 [2, 768, 768], replicated
- w_value: bfloat16 [2, 768, 768], replicated
- w_attn_out: bfloat16 [2, 768, 768], replicated
- w_router: float32 [2, 768, 32], replicated
- w_in: bfloat16 [2, 32, 768, 3072], P(None, 'ep')
- w_out: bfloat16 [2, 32, 3072, 768], P(None, 'ep')
Outputs:
- output: bfloat16 [384, 384, 768], P(('dp', 'ep')), parts along dimension 0
There are 4 independent parts. A program takes and returns all parts, laid end to end along the dimension named above; an argument that names none is the same for every part.
All inputs are finite; a program needn't handle non-finite values.
Results may differ from a plain program's by a relative error of at most 0.0195101.
Values are sent between devices in bfloat16 or wider.
A program may use at most 768 MiB of HBM per device.

v0:
```python
import jax
import jax.numpy as jnp
from jax import lax
from jax.sharding import PartitionSpec as P, NamedSharding

NORM_EPS = 1e-6
NEG_BIG = -1e9
CAP_FACTOR = 2


def rms_norm(hidden, gain):
    hid32 = hidden.astype(jnp.float32)
    return hid32 * lax.rsqrt(jnp.mean(hid32 * hid32, axis=-1, keepdims=True) + NORM_EPS) * gain


def attention(hidden, pad_mask, rel_bias, gain, query_w, key_w, value_w, out_w):
    num_seqs, seq_len, model_dim = hidden.shape
    num_heads = rel_bias.shape[0]
    head_dim = query_w.shape[1] // num_heads
    normed = rms_norm(hidden, gain).astype(jnp.bfloat16)

    def project(weight):
        out_rows = jnp.einsum('std,de->ste', normed, weight, preferred_element_type=jnp.float32)
        return out_rows.astype(jnp.bfloat16).reshape(num_seqs, seq_len, num_heads, head_dim)

    query_rows = project(query_w)
    key_rows = project(key_w)
    value_rows = project(value_w)
    scores = jnp.einsum('sqhd,skhd->shqk', query_rows, key_rows, preferred_element_type=jnp.float32)
    scores = scores + rel_bias[None] + jnp.where(pad_mask > 0, 0.0, NEG_BIG)[:, None, None, :]
    attn_probs = jax.nn.softmax(scores, axis=-1).astype(jnp.bfloat16)
    context = jnp.einsum('shqk,skhd->sqhd', attn_probs, value_rows, preferred_element_type=jnp.float32)
    context = context.astype(jnp.bfloat16).reshape(num_seqs, seq_len, num_heads * head_dim)
    attn_out = jnp.einsum('ste,ed->std', context, out_w, preferred_element_type=jnp.float32)
    return (hidden.astype(jnp.float32) + attn_out).astype(jnp.bfloat16)


def token_slots(expert_ids, num_experts):
    tok_count = expert_ids.shape[0]
    sort_order = jnp.argsort(expert_ids, stable=True)
    counts = jnp.zeros((num_experts,), jnp.int32).at[expert_ids].add(1)
    starts = jnp.cumsum(counts) - counts
    rank_sorted = jnp.arange(tok_count, dtype=jnp.int32) - starts[expert_ids[sort_order]]
    return jnp.zeros((tok_count,), jnp.int32).at[sort_order].set(rank_sorted)


def dispatch(flat_hidden, expert_ids, gain, route_w, capacity):
    tok_count, model_dim = flat_hidden.shape
    num_experts = route_w.shape[1]
    normed32 = rms_norm(flat_hidden, gain)
    logits = jnp.dot(normed32, route_w, precision=lax.Precision.HIGHEST, preferred_element_type=jnp.float32)
    gate_val = jnp.take_along_axis(jax.nn.softmax(logits, axis=-1), expert_ids[:, None], axis=1)[:, 0]
    token_slot = token_slots(expert_ids, num_experts)
    flat_slot = jnp.where(token_slot < capacity, expert_ids * capacity + token_slot, num_experts * capacity)
    slot_token = jnp.full((num_experts * capacity,), tok_count, jnp.int32).at[flat_slot].set(jnp.arange(tok_count, dtype=jnp.int32), mode='drop')
    packed = jnp.take(normed32.astype(jnp.bfloat16), slot_token, axis=0, mode='fill', fill_value=0)
    return packed.reshape(num_experts, capacity, model_dim), gate_val, flat_slot


def expert_ffn(rows_in, up_w, down_w):
    inner_act = jnp.einsum('ecd,edf->ecf', rows_in, up_w, preferred_element_type=jnp.float32)
    inner_act = jnp.maximum(inner_act, 0.0).astype(jnp.bfloat16)
    return jnp.einsum('ecf,efd->ecd', inner_act, down_w, preferred_element_type=jnp.float32).astype(jnp.bfloat16)


def combine(flat_hidden, expert_rows, gate_val, flat_slot):
    returned = jnp.take(expert_rows, flat_slot, axis=0, mode='fill', fill_value=0)
    return (flat_hidden.astype(jnp.float32) + gate_val[:, None] * returned.astype(jnp.float32)).astype(jnp.bfloat16)


def solution(mesh):
    token_spec = P(('dp', 'ep'))

    def per_device(x_in, pad_mask, rel_bias, expert_idx, norm_scale, w_query, w_key, w_value, w_attn_out, w_router, w_in, w_out):
        num_seqs, seq_len, model_dim = x_in.shape
        tok_count = num_seqs * seq_len
        num_experts = w_router.shape[2]
        capacity = (CAP_FACTOR * tok_count + num_experts - 1) // num_experts
        hidden = x_in
        for layer_id in range(w_router.shape[0]):
            hidden = attention(hidden, pad_mask, rel_bias, norm_scale[layer_id, 0], w_query[layer_id], w_key[layer_id], w_value[layer_id], w_attn_out[layer_id])
            flat_hidden = hidden.reshape(tok_count, model_dim)
            packed, gate_val, flat_slot = dispatch(flat_hidden, expert_idx[layer_id].reshape(tok_count), norm_scale[layer_id, 1], w_router[layer_id], capacity)
            received = lax.all_to_all(packed, 'ep', 0, 1, tiled=True)
            expert_rows = expert_ffn(received, w_in[layer_id], w_out[layer_id])
            returned = lax.all_to_all(expert_rows, 'ep', 1, 0, tiled=True)
            hidden = combine(flat_hidden, returned.reshape(num_experts * capacity, model_dim), gate_val, flat_slot).reshape(num_seqs, seq_len, model_dim)
        return hidden

    return jax.shard_map(per_device, mesh=mesh, in_specs=(token_spec, token_spec, P(), P(None, ('dp', 'ep')), P(), P(), P(), P(), P(), P(), P(None, 'ep'), P(None, 'ep')), out_specs=token_spec, check_vma=False)
```

profile of v0, /device:TPU:81, one launch (start us, length us, event | category | flops | bytes accessed | tf_op | source)
XLA Modules:
  0.0 1637.0 jit_solution(7182466772911874754)
XLA Ops:
  3.5 32.3 %scatter_custom_fusion = s32[32]{0:T(128)S(1)} fusion(s32[4608]{0:T(1024)S(1)} %get-tuple-element.85, s32[4608]{0:T(1024)S(1)} %broadcast.368, s32[]{:T(128)} %constant.38.clone.1), kind=kCustom, calls=%fused_computation.238 | custom fusion | flops 4608 | bytes 132 | tf_op jit(solution)/shard_map/scatter-add | solution.py:41
  44.3 24.1 %gather_fusion = s32[4608]{0:T(1024)S(1)} fusion(s32[4608]{0:T(1024)S(1)} %reshape_squeeze.6, s32[5120]{0:T(1024)S(1)} %pad_clamp_fusion.3), kind=kCustom, calls=%fused_computation.6 | custom fusion | bytes 55296 | tf_op jit(solution)/shard_map/gather | solution.py:43
  201.5 43.7 %fusion.123 = (f32[12,12,384]{2,1,0:T(8,128)S(1)}, f32[12,12,384,384]{2,3,1,0:T(8,128)}) fusion(f32[12,384]{1,0:T(8,128)S(1)} %compare_select_fusion.22, f32[12,384,384]{1,2,0:T(8,128)} %copy.63, bf16[12,384,12,64]{1,3,2,0:T(8,128)(2,1)} %bitcast.256, bf16[12,384,12,64]{1,3,2,0:T(8,128)(2,1)} %bitcast.257), kind=kOutput, calls=%fused_computation.252 | convolution fusion | flops 2802843904 | bytes 106407936 | tf_op jit(solution)/shard_map/sub | solution.py:31
  245.2 32.3 %fusion.54 = bf16[12,12,64,384]{3,2,1,0:T(8,128)(2,1)} fusion(bf16[12,384,12,64]{1,3,2,0:T(8,128)(2,1)} %bitcast.263, f32[12,12,384,384]{2,3,1,0:T(8,128)} %get-tuple-element.151, f32[12,12,384]{2,1,0:T(8,128)S(1)} %get-tuple-element.150), kind=kOutput, calls=%fused_computation.84 | convolution fusion | flops 2763915264 | bytes 99311616 | tf_op jit(solution)/shard_map/shqk,skhd->sqhd/dot_general | solution.py:32
  296.4 45.6 %gather_fusion.3 = bf16[9216,768]{1,0:T(8,128)(2,1)} fusion(bf16[4608,768]{1,0:T(8,128)(2,1)} %fusion.36, s32[9216]{0:T(1024)S(1)} %copy-done.14), kind=kCustom, calls=%fused_computation.1.clone | custom fusion | bytes 28348416 | tf_op jit(solution)/shard_map/jit(_take)/gather | solution.py:56
  351.1 161.2 %all_to_all.66 = bf16[32,288,768]{2,1,0:T(8,128)(2,1)S(1)} all-to-all(bf16[32,288,768]{2,1,0:T(8,128)(2,1)S(1)} %bitcast.251), channel_id=1, replica_groups=mesh['dp'=4,'ep'=8] {'ep'}, dimensions={0} | all-to-all | bytes 28311552 | tf_op jit(solution)/shard_map/all_to_all | solution.py:84
  517.8 53.0 %maximum_convert_fusion.1.clone.7 = bf16[4,2304,3072]{2,1,0:T(8,128)(2,1)} fusion(bf16[4,2304,768]{2,1,0:T(8,128)(2,1)} %bitcast.260, bf16[2,4,768,3072]{3,2,1,0:T(8,128)(2,1)} %param.28), kind=kOutput, calls=%fused_computation.17.clone.clone.clone.clone.clone.2 | convolution fusion | flops 43543166976 | bytes 89653248 | tf_op jit(solution)/shard_map/ecd,edf->ecf/dot_general | solution.py:61
  570.8 51.1 %fusion.43 = bf16[4,2304,768]{2,1,0:T(8,128)(2,1)} fusion(bf16[2,4,3072,768]{3,2,1,0:T(8,128)(2,1)} %param.29, bf16[4,2304,3072]{2,1,0:T(8,128)(2,1)} %maximum_convert_fusion.1.clone.7), kind=kOutput, calls=%fused_computation.73 | convolution fusion | flops 43493621760 | bytes 89653248 | tf_op jit(solution)/shard_map/ecf,efd->ecd/dot_general | solution.py:63
  621.9 38.2 %copy.68 = bf16[4,2304,768]{2,0,1:T(4,128)(2,1)} copy(bf16[4,2304,768]{2,1,0:T(8,128)(2,1)} %fusion.43) | data formatting | bytes 28311552 | tf_op jit(solution)/shard_map/convert_element_type | solution.py:63
  673.6 24.1 %gather_fusion.1 = s32[4608]{0:T(1024)S(1)} fusion(s32[4608]{0:T(1024)S(1)} %reshape_squeeze.7, s32[5120]{0:T(1024)S(1)} %pad_clamp_fusion.1), kind=kCustom, calls=%fused_computation.7 | custom fusion | bytes 55296 | tf_op jit(solution)/shard_map/gather | solution.py:43
  697.7 32.6 %scatter_custom_fusion.3 = s32[32]{0:T(128)S(1)} fusion(s32[4608]{0:T(1024)} %get-tuple-element.162, s32[4608]{0:T(1024)} %copy-done.31, s32[]{:T(128)} %constant.38.clone.1), kind=kCustom, calls=%fused_computation.236 | custom fusion | flops 4608 | bytes 640 | tf_op jit(solution)/shard_map/scatter-add | solution.py:41
  771.7 17.6 %scatter_custom_fusion.5 = s32[9216]{0:T(1024)S(1)} fusion(s32[4608]{0:T(1024)S(1)} %get-tuple-element.69, s32[4608]{0:T(1024)S(1)} %iota.24, s32[]{:T(128)} %constant.15.clone.1), kind=kCustom, calls=%fused_computation.220 | custom fusion | bytes 36868 | tf_op jit(solution)/shard_map/scatter | solution.py:55
  815.8 37.1 %gather_fusion.2 = f32[4608]{0:T(1024)S(1)} fusion(f32[4608,32]{0,1:T(8,128)S(1)} %fusion.74, s32[4608]{0:T(1024)S(1)} %fusion.100), kind=kCustom, calls=%fused_computation.clone | custom fusion | bytes 73728 | tf_op jit(solution)/shard_map/jit(take_along_axis)/gather | solution.py:52
  865.6 24.4 %gather_fusion.4 = bf16[4608,768]{1,0:T(8,128)(2,1)} fusion(bf16[9216,768]{1,0:T(8,128)(2,1)} %bitcast.247, s32[5120]{0:T(1024)S(1)} %pad_clamp_fusion.2), kind=kCustom, calls=%fused_computation.2.clone | custom fusion | bytes 14174208 | tf_op jit(solution)/shard_map/jit(_take)/gather | solution.py:67
  969.0 43.5 %fusion.125 = (f32[12,12,384]{2,1,0:T(8,128)S(1)}, f32[12,12,384,384]{2,3,1,0:T(8,128)}) fusion(f32[12,384]{1,0:T(8,128)S(1)} %copy-done.2, f32[12,384,384]{1,2,0:T(8,128)} %copy.63, bf16[12,384,12,64]{1,3,2,0:T(8,128)(2,1)} %bitcast.259, bf16[12,384,12,64]{1,3,2,0:T(8,128)(2,1)} %bitcast.258), kind=kOutput, calls=%fused_computation.254 | convolution fusion | flops 2802843904 | bytes 106407936 | tf_op jit(solution)/shard_map/sub | solution.py:31
  1012.5 32.3 %fusion.53 = bf16[12,12,64,384]{3,2,1,0:T(8,128)(2,1)} fusion(bf16[12,384,12,64]{1,3,2,0:T(8,128)(2,1)} %bitcast.262, f32[12,12,384,384]{2,3,1,0:T(8,128)} %get-tuple-element.157, f32[12,12,384]{2,1,0:T(8,128)S(1)} %get-tuple-element.156), kind=kOutput, calls=%fused_computation.83 | convolution fusion | flops 2763915264 | bytes 99311616 | tf_op jit(solution)/shard_map/shqk,skhd->sqhd/dot_general | solution.py:32
  1066.7 45.6 %gather_fusion.6 = bf16[9216,768]{1,0:T(8,128)(2,1)} fusion(bf16[4608,768]{1,0:T(8,128)(2,1)} %fusion.31, s32[9216]{0:T(1024)S(1)} %copy-done.13), kind=kCustom, calls=%fused_computation.4.clone | custom fusion | bytes 28348416 | tf_op jit(solution)/shard_map/jit(_take)/gather | solution.py:56
  1121.4 160.5 %all_to_all.67 = bf16[32,288,768]{2,1,0:T(8,128)(2,1)S(1)} all-to-all(bf16[32,288,768]{2,1,0:T(8,128)(2,1)S(1)} %bitcast.252), channel_id=1, replica_groups=mesh['dp'=4,'ep'=8] {'ep'}, dimensions={0} | all-to-all | bytes 28311552 | tf_op jit(solution)/shard_map/all_to_all | solution.py:84
  1287.4 53.0 %maximum_convert_fusion.clone.7 = bf16[4,2304,3072]{2,1,0:T(8,128)(2,1)} fusion(bf16[4,2304,768]{2,1,0:T(8,128)(2,1)} %bitcast.261, bf16[2,4,768,3072]{3,2,1,0:T(8,128)(2,1)} %param.28), kind=kOutput, calls=%fused_computation.16.clone.clone.clone.clone.clone.2 | convolution fusion | flops 43543166976 | bytes 89653248 | tf_op jit(solution)/shard_map/ecd,edf->ecf/dot_general | solution.py:61
  1340.5 51.1 %fusion.38 = bf16[4,2304,768]{2,1,0:T(8,128)(2,1)} fusion(bf16[2,4,3072,768]{3,2,1,0:T(8,128)(2,1)} %param.29, bf16[4,2304,3072]{2,1,0:T(8,128)(2,1)} %maximum_convert_fusion.clone.7), kind=kOutput, calls=%fused_computation.72 | convolution fusion | flops 43493621760 | bytes 89653248 | tf_op jit(solution)/shard_map/ecf,efd->ecd/dot_general | solution.py:63
  1391.6 38.0 %copy.77 = bf16[4,2304,768]{2,0,1:T(4,128)(2,1)} copy(bf16[4,2304,768]{2,1,0:T(8,128)(2,1)} %fusion.38) | data formatting | bytes 28311552 | tf_op jit(solution)/shard_map/convert_element_type | solution.py:63
  1462.4 37.1 %gather_fusion.5 = f32[4608]{0:T(1024)S(1)} fusion(f32[4608,32]{0,1:T(8,128)S(1)} %fusion.76, s32[4608]{0:T(1024)S(1)} %fusion.101), kind=kCustom, calls=%fused_computation.3.clone | custom fusion | bytes 73728 | tf_op jit(solution)/shard_map/jit(take_along_axis)/gather | solution.py:52
  1499.6 92.2 %all-to-all-done.3 = bf16[4,2304,768]{2,0,1:T(4,128)(2,1)} async-done(((bf16[4,2304,768]{2,0,1:T(4,128)(2,1)}), bf16[4,2304,768]{2,0,1:T(4,128)(2,1)}, u32[]{:S(2)}, u32[]{:S(2)}) %all-to-all-start.3) | async-done | bytes 14155808 | tf_op jit(solution)/shard_map/all_to_all | solution.py:86
  1603.2 24.4 %gather_fusion.7 = bf16[4608,768]{1,0:T(8,128)(2,1)} fusion(bf16[9216,768]{1,0:T(8,128)(2,1)} %bitcast.248, s32[5120]{0:T(1024)S(1)} %pad_clamp_fusion), kind=kCustom, calls=%fused_computation.5.clone | custom fusion | bytes 14174208 | tf_op jit(solution)/shard_map/jit(_take)/gather | solution.py:67
  (185 shorter events, 441.1 us)
Async XLA Ops:
  0.0 127.2 %copy-start.34 = (f32[2,2,768]{2,1,0:T(2,128)S(1)}, f32[2,2,768]{2,1,0:T(2,128)}, u32[]{:S(2)}) copy-start(f32[2,2,768]{2,1,0:T(2,128)} %param.22) | copy-start | bytes 36868
  0.0 127.8 %copy-start.29 = (s32[12,384]{1,0:T(8,128)S(1)}, s32[12,384]{1,0:T(8,128)}, u32[]{:S(2)}) copy-start(s32[12,384]{1,0:T(8,128)} %param.19) | copy-start | bytes 55300
  3.4 32.3 %copy-start.31 = (s32[4608]{0:T(1024)}, s32[4608]{0:T(1024)S(1)}, u32[]{:S(2)}) copy-start(s32[4608]{0:T(1024)S(1)} %broadcast.368) | copy-start | bytes 55300
  68.4 72.0 %copy-start.37 = (bf16[2,768,768]{2,1,0:T(8,128)(2,1)S(1)}, bf16[2,768,768]{2,1,0:T(8,128)(2,1)}, u32[]{:S(2)}) copy-start(bf16[2,768,768]{2,1,0:T(8,128)(2,1)} %param.23) | copy-start | bytes 7077892
  108.4 42.0 %copy-start.17 = (s32[4608]{0:T(1024)}, s32[4608]{0:T(1024)S(1)}, u32[]{:S(2)}) copy-start(s32[4608]{0:T(1024)S(1)} %get-tuple-element.75) | copy-start | bytes 55300
  127.8 73.7 %copy-start.1 = (f32[12,384]{1,0:T(8,128)}, f32[12,384]{1,0:T(8,128)S(1)}, u32[]{:S(2)}) copy-start(f32[12,384]{1,0:T(8,128)S(1)} %compare_select_fusion.22) | copy-start | bytes 55300
  201.5 76.0 %slice-start = ((s8[7077888]{0:T(1024)(128)(4,1)}), s8[2883584]{0:T(1024)(128)(4,1)S(1)}, s32[]{:S(2)}) async-start(s8[7077888]{0:T(1024)(128)(4,1)} %bitcast.267), calls=%async_computation.4 | async-start | bytes 5767168
  245.2 32.3 %slice-start.1 = ((s8[7077888]{0:T(1024)(128)(4,1)}), s8[4194304]{0:T(1024)(128)(4,1)S(1)}, s32[]{:S(2)}) async-start(s8[7077888]{0:T(1024)(128)(4,1)} %bitcast.267), calls=%async_computation.5 | async-start | bytes 8388608
  288.7 53.2 %copy-start.3 = (f32[12,384]{1,0:T(8,128)}, f32[12,384]{1,0:T(8,128)S(1)}, u32[]{:S(2)}) copy-start(f32[12,384]{1,0:T(8,128)S(1)} %add_rsqrt_fusion.1) | copy-start | bytes 55300
  296.4 45.6 %copy-start.24 = (pred[9216]{0:T(1024)(128)(4,1)S(1)}, pred[9216]{0:T(1024)(128)(4,1)}, u32[]{:S(2)}) copy-start(pred[9216]{0:T(1024)(128)(4,1)} %compare_and_fusion.1) | copy-start | bytes 27652
  660.2 194.1 %all-to-all-start.1 = ((bf16[4,2304,768]{2,0,1:T(4,128)(2,1)}), bf16[4,2304,768]{2,0,1:T(4,128)(2,1)}, u32[]{:S(2)}, u32[]{:S(2)}) async-start(bf16[4,2304,768]{2,0,1:T(4,128)(2,1)} %copy.68), calls=%async_computation.1 | async-start | bytes 28311552 | tf_op jit(solution)/shard_map/all_to_all | solution.py:86
  666.7 122.6 %copy-start.21 = (s32[4608,1,1]{0,2,1:T(1,128)S(1)}, s32[4608,1,1]{0,2,1:T(1,128)}, u32[]{:S(2)}) copy-start(s32[4608,1,1]{0,2,1:T(1,128)} %get-tuple-element.84) | copy-start | bytes 55300
  666.7 122.6 %copy-start.22 = (s32[4608,1,1]{0,2,1:T(1,128)S(1)}, s32[4608,1,1]{0,2,1:T(1,128)}, u32[]{:S(2)}) copy-start(s32[4608,1,1]{0,2,1:T(1,128)} %get-tuple-element.163) | copy-start | bytes 55300
  666.7 123.3 %copy-start.4 = (f32[12,384]{1,0:T(8,128)S(1)}, f32[12,384]{1,0:T(8,128)}, u32[]{:S(2)}) copy-start(f32[12,384]{1,0:T(8,128)} %copy-done.3) | copy-start | bytes 55300
  666.7 123.3 %copy-start.28 = (f32[768]{0:T(1024)S(1)}, f32[768]{0:T(1024)}, u32[]{:S(2)}) copy-start(f32[768]{0:T(1024)} %get-tuple-element.65) | copy-start | bytes 9220
  697.7 101.8 %copy-start.7 = (f32[2,768,32]{1,2,0:T(8,128)S(1)}, f32[2,768,32]{1,2,0:T(8,128)}, u32[]{:S(2)}) copy-start(f32[2,768,32]{1,2,0:T(8,128)} %param.27) | copy-start | bytes 589828
  815.5 37.4 %copy-start.18 = (s32[4608]{0:T(1024)S(1)}, s32[4608]{0:T(1024)}, u32[]{:S(2)}) copy-start(s32[4608]{0:T(1024)} %copy-done.17) | copy-start | bytes 55300
  815.5 37.4 %copy-start.12 = (s32[1,12,384]{2,0,1:T(1,128)S(1)}, s32[1,12,384]{2,0,1:T(1,128)}, u32[]{:S(2)}) copy-start(s32[1,12,384]{2,0,1:T(1,128)} %copy-done.11) | copy-start | bytes 55300
  865.6 24.4 %copy-start.30 = (pred[4608]{0:T(1024)(128)(4,1)S(1)}, pred[4608]{0:T(1024)(128)(4,1)}, u32[]{:S(2)}) copy-start(pred[4608]{0:T(1024)(128)(4,1)} %get-tuple-element.74) | copy-start | bytes 13828
  1012.5 32.3 %copy-start.41 = (bf16[2,768,768]{2,1,0:T(8,128)(2,1)S(1)}, bf16[2,768,768]{2,1,0:T(8,128)(2,1)}, u32[]{:S(2)}) copy-start(bf16[2,768,768]{2,1,0:T(8,128)(2,1)} %param.26) | copy-start | bytes 7077892
  1059.0 53.2 %copy-start.5 = (f32[12,384]{1,0:T(8,128)}, f32[12,384]{1,0:T(8,128)S(1)}, u32[]{:S(2)}) copy-start(f32[12,384]{1,0:T(8,128)S(1)} %add_rsqrt_fusion) | copy-start | bytes 55300
  1066.7 45.6 %copy-start.23 = (pred[9216]{0:T(1024)(128)(4,1)S(1)}, pred[9216]{0:T(1024)(128)(4,1)}, u32[]{:S(2)}) copy-start(pred[9216]{0:T(1024)(128)(4,1)} %compare_and_fusion) | copy-start | bytes 27652
  1429.7 162.2 %all-to-all-start.3 = ((bf16[4,2304,768]{2,0,1:T(4,128)(2,1)}), bf16[4,2304,768]{2,0,1:T(4,128)(2,1)}, u32[]{:S(2)}, u32[]{:S(2)}) async-start(bf16[4,2304,768]{2,0,1:T(4,128)(2,1)} %copy.77), calls=%async_computation.3 | async-start | bytes 28311552 | tf_op jit(solution)/shard_map/all_to_all | solution.py:86
  1462.1 37.4 %copy-start.10 = (s32[1,12,384]{2,0,1:T(1,128)S(1)}, s32[1,12,384]{2,0,1:T(1,128)}, u32[]{:S(2)}) copy-start(s32[1,12,384]{2,0,1:T(1,128)} %copy-done.9) | copy-start | bytes 55300
  (22 other events, 222.2 us)
where the time goes:
time: 1650 us; the launch traced here: 1640 us
  local copies, waits for them, and re-layouts  518 us (31%)
  matrix products  474 us (29%)
  blocking collectives  322 us (20%)
  other arithmetic  217 us (13%)
  waiting for transfers between devices  92.2 us (6%)
    all_to_all x2, blocking collectives, per_device(): received = lax.all_to_all(packed, 'ep', 0, 1, tiled=True)  322 us
    dot_general x2, matrix products, expert_ffn(): jnp.einsum('ecd,edf->ecf', rows_in, up_w, preferred_element_type=jnp.floa...  106 us
    dot_general x2, matrix products, expert_ffn(): jnp.einsum('ecf,efd->ecd', inner_act, down_w, preferred_element_type=jnp....  102 us
    all_to_all x2, waiting for transfers between devices, per_device(): returned = lax.all_to_all(expert_rows, 'ep', 1, 0, tiled=True)  92.2 us
    gather x2, local copies, waits for them, and re-layouts, dispatch(): jnp.take(normed32.astype(jnp.bfloat16), slot_token, axis=0, mode='fill',...  91.1 us
    sub x2, matrix products, attention(): attn_probs = jax.nn.softmax(scores, axis=-1).astype(jnp.bfloat16)  87.3 us
    convert_element_type x2, local copies, waits for them, and re-layouts, expert_ffn(): jnp.einsum('ecf,efd->ecd', inner_act, down_w, preferred_element_type=jnp....  76.3 us
    gather x2, local copies, waits for them, and re-layouts, dispatch(): jnp.take_along_axis(jax.nn.softmax(logits, axis=-1), expert_ids[:, None],...  74.2 us
  transfers between devices with their start and end apart: 2, of which 1 were waited for; matrix products, arithmetic and copies ran while one was open for 15% of the time, Pallas kernels for 0%

commit v1 on v0

v1 whole, which is shorter than its diff:
```python
import functools

import jax
import jax.numpy as jnp
from jax import lax
from jax.experimental import pallas as pl
from jax.experimental.pallas import tpu as pltpu
from jax.sharding import PartitionSpec as P

NORM_EPS = 1e-6
NEG_BIG = -1e9
CAP_FACTOR = 2
LANES = 128
MESH = pl.DeviceIdType.MESH
f32 = jnp.float32
bf16 = jnp.bfloat16


def routing_kernel(capacity, ids_ref, place_ref, token_ref):
    num_experts = token_ref.shape[1]
    tok_count = ids_ref.shape[2]
    expert = lax.broadcasted_iota(jnp.int32, (num_experts, LANES), 0)
    upper = (lax.broadcasted_iota(jnp.int32, (LANES, LANES), 0) <= lax.broadcasted_iota(jnp.int32, (LANES, LANES), 1)).astype(bf16)
    lane = lax.broadcasted_iota(jnp.int32, (1, LANES), 1).astype(f32)
    slot_rows = lax.broadcasted_iota(jnp.int32, (capacity, LANES), 0)
    seen = jnp.zeros((num_experts, 1), f32)
    low = jnp.zeros((num_experts, capacity), f32)
    high = jnp.zeros((num_experts, capacity), f32)
    for blk in range(tok_count // LANES):
        span = slice(blk * LANES, (blk + 1) * LANES)
        ids = ids_ref[0, :, span]
        hot = jnp.where(expert == ids, 1.0, 0.0)
        count = jnp.dot(hot.astype(bf16), upper, preferred_element_type=f32) + seen
        slot = jnp.sum(hot * count, axis=0, keepdims=True).astype(jnp.int32) - 1
        seen = count[:, LANES - 1:]
        place_ref[0, :, span] = jnp.where(slot < capacity, ids * capacity + slot, -1)
        in_slot = jnp.where(slot_rows == slot, 1.0, 0.0).astype(bf16)
        dims = (((1,), (1,)), ((), ()))
        low = low + lax.dot_general((hot * lane).astype(bf16), in_slot, dims, preferred_element_type=f32)
        high = high + blk * lax.dot_general(hot.astype(bf16), in_slot, dims, preferred_element_type=f32)
    token_ref[0] = (high * LANES + low).astype(jnp.int32)


def routing(ids, num_experts, capacity):
    layers, _, tok_count = ids.shape
    row = pl.BlockSpec((1, 1, tok_count), lambda i: (i, 0, 0))
    return pl.pallas_call(
        functools.partial(routing_kernel, capacity),
        grid=(layers,),
        in_specs=[row],
        out_specs=[row, pl.BlockSpec((1, num_experts, capacity), lambda i: (i, 0, 0))],
        out_shape=[jax.ShapeDtypeStruct((layers, 1, tok_count), jnp.int32), jax.ShapeDtypeStruct((layers, num_experts, capacity), jnp.int32)],
        name="routing",
    )(ids)


def split_router(weight):
    hi = lax.reduce_precision(weight, 8, 7)
    mid = lax.reduce_precision(weight - hi, 8, 7)
    lo = lax.reduce_precision(weight - hi - mid, 8, 7)
    pad = jnp.zeros(weight.shape[:-1] + (LANES - 3 * weight.shape[-1],), weight.dtype)
    return jnp.concatenate([hi, mid, lo, pad], axis=-1).astype(bf16)


def attention_kernel(num_experts, x_ref, mask_ref, bias_ref, gain_ref, wq_ref, wk_ref, wv_ref, wo_ref, wr_ref, ids_ref, h1_ref, b_ref, gate_ref, ctx_ref):
    seq_len, model_dim = x_ref.shape[1:]
    num_heads = bias_ref.shape[0]
    head_dim = ctx_ref.shape[1] // num_heads
    gains = gain_ref[0]
    x = x_ref[0].astype(f32)
    a = (x * lax.rsqrt(jnp.mean(x * x, axis=-1, keepdims=True) + NORM_EPS) * gains[0:1]).astype(bf16)
    q = jnp.dot(a, wq_ref[0], preferred_element_type=f32).astype(bf16)
    k = jnp.dot(a, wk_ref[0], preferred_element_type=f32).astype(bf16)
    v = jnp.dot(a, wv_ref[0], preferred_element_type=f32).astype(bf16)
    mask_add = jnp.where(mask_ref[0] > 0, 0.0, NEG_BIG)
    first = lax.broadcasted_iota(jnp.int32, (seq_len, 2 * head_dim), 1) < head_dim
    zero = jnp.zeros((seq_len, 2 * head_dim), bf16)

    def probs(scores, head):
        scores = scores + bias_ref[head] + mask_add
        e = jnp.exp(scores - jnp.max(scores, axis=-1, keepdims=True))
        return (e * (1.0 / jnp.sum(e, axis=-1, keepdims=True))).astype(bf16)

    for pair in range(num_heads // 2):
        lanes = slice(2 * head_dim * pair, 2 * head_dim * (pair + 1))
        kp, vp = k[:, lanes], v[:, lanes]
        keys = jnp.concatenate([jnp.where(first, kp, zero), jnp.where(first, zero, kp)], axis=0)
        values = jnp.concatenate([jnp.where(first, vp, zero), jnp.where(first, zero, vp)], axis=0)
        s = lax.dot_general(q[:, lanes], keys, (((1,), (1,)), ((), ())), preferred_element_type=f32)
        p = jnp.concatenate([probs(s[:, :seq_len], 2 * pair), probs(s[:, seq_len:], 2 * pair + 1)], axis=1)
        ctx_ref[:, lanes] = jnp.dot(p, values, preferred_element_type=f32).astype(bf16)
    h1 = (x + jnp.dot(ctx_ref[...], wo_ref[0], preferred_element_type=f32)).astype(bf16)
    h1_ref[0] = h1
    h = h1.astype(f32)
    r = h * lax.rsqrt(jnp.mean(h * h, axis=-1, keepdims=True) + NORM_EPS) * gains[1:2]
    b = r.astype(bf16)
    b_ref[0] = b
    rest = r - b.astype(f32)
    mid = rest.astype(bf16)
    tail = (rest - mid.astype(f32)).astype(bf16)
    wr = wr_ref[0]
    lane = lax.broadcasted_iota(jnp.int32, (1, LANES), 1)
    part0 = jnp.dot(b, wr, preferred_element_type=f32)
    part1 = jnp.dot(mid, wr, preferred_element_type=f32)
    part2 = jnp.dot(tail, wr, preferred_element_type=f32)
    parts = part0 + jnp.where(lane < 2 * num_experts, part1, 0.0) + jnp.where(lane < num_experts, part2, 0.0)
    parts = parts.T
    logits = parts[:num_experts] + (parts[num_experts:2 * num_experts] + parts[2 * num_experts:3 * num_experts])
    e = jnp.exp(logits - jnp.max(logits, axis=0, keepdims=True))
    chosen = lax.broadcasted_iota(jnp.int32, (num_experts, seq_len), 0) == ids_ref[0, 0]
    gate_ref[0] = jnp.sum(jnp.where(chosen, e, 0.0), axis=0, keepdims=True) / jnp.sum(e, axis=0, keepdims=True)


def attention(layer, num_experts, x, mask, bias, ids, gains, wq, wk, wv, wo, wr):
    num_seqs, seq_len, model_dim = x.shape
    num_heads = bias.shape[0]
    inner = wq.shape[2]
    once = pl.Buffered(1)
    rows = pl.BlockSpec((1, seq_len, model_dim), lambda i: (i, 0, 0))
    line = pl.BlockSpec((1, 1, seq_len), lambda i: (i, 0, 0))

    def of_layer(array):
        return pl.BlockSpec((1,) + array.shape[1:], lambda i: (layer, 0, 0), pipeline_mode=once)

    flops = 2 * num_seqs * seq_len * (4 * model_dim * inner + 2 * seq_len * inner)
    return pl.pallas_call(
        functools.partial(attention_kernel, num_experts),
        grid=(num_seqs,),
        in_specs=[rows, line, pl.BlockSpec(bias.shape, lambda i: (0, 0, 0), pipeline_mode=once), of_layer(gains), of_layer(wq), of_layer(wk), of_layer(wv), of_layer(wo), of_layer(wr), pl.BlockSpec((1, 1, 1, seq_len), lambda i: (layer, i, 0, 0))],
        out_specs=[rows, rows, line],
        out_shape=[jax.ShapeDtypeStruct(x.shape, bf16), jax.ShapeDtypeStruct(x.shape, bf16), jax.ShapeDtypeStruct((num_seqs, 1, seq_len), f32)],
        scratch_shapes=[pltpu.VMEM((seq_len, inner), bf16)],
        compiler_params=pltpu.CompilerParams(vmem_limit_bytes=56 * 2**20),
        cost_estimate=pl.CostEstimate(flops=flops, bytes_accessed=8 * num_seqs * seq_len * model_dim, transcendentals=num_seqs * num_heads * seq_len * seq_len),
        name="attention",
    )(x, mask, bias, gains, wq, wk, wv, wo, wr, ids)


def exchange_kernel(layer, n, packed_ref, w_in_ref, w_out_ref, out_ref, rows, hid, up, down, load_sem, send_sem, recv_sem, ret_send, ret_recv, own_sem):
    local, _, cap, dim = rows.shape
    ff = up.shape[2]
    per = hid.shape[0] // cap
    me = lax.axis_index("ep")
    order = sorted(range(1, n), key=lambda k: abs(k - n // 2))

    def load(j):
        return (
            pltpu.make_async_copy(w_in_ref.at[layer, j], up.at[j % 2], load_sem.at[j % 2, 0]),
            pltpu.make_async_copy(w_out_ref.at[layer, j], down.at[j % 2], load_sem.at[j % 2, 1]),
        )

    def send(j, k):
        peer = lax.rem(me + k, n)
        return pltpu.make_async_remote_copy(
            src_ref=packed_ref.at[peer * local + j],
            dst_ref=rows.at[j, me],
            send_sem=send_sem.at[j, k],
            recv_sem=recv_sem.at[j, k],
            device_id={"ep": peer},
            device_id_type=MESH,
        )

    def send_back(j, k):
        peer = lax.rem(me + k, n)
        return pltpu.make_async_remote_copy(
            src_ref=rows.at[j, peer],
            dst_ref=out_ref.at[me * local + j],
            send_sem=ret_send.at[j, k],
            recv_sem=ret_recv.at[j, k],
            device_id={"ep": peer},
            device_id_type=MESH,
        )

    for c in load(0):
        c.start()
    barrier = pltpu.get_barrier_semaphore()
    for k in range(1, n):
        pl.semaphore_signal(barrier, inc=1, device_id={"ep": lax.rem(me + k, n)}, device_id_type=MESH)
    pl.semaphore_wait(barrier, n - 1)
    own_in = [pltpu.make_async_copy(packed_ref.at[me * local + j], rows.at[j, me], own_sem.at[0, j]) for j in range(local)]
    own_out = [pltpu.make_async_copy(rows.at[j, me], out_ref.at[me * local + j], own_sem.at[1, j]) for j in range(local)]
    for j in range(local):
        for k in order:
            send(j, k).start()
        own_in[j].start()
    for j in range(local):
        for c in load(j):
            c.wait()
        if j + 1 < local:
            for c in load(j + 1):
                c.start()
        own_in[j].wait()
        for k in order:
            send(j, k).wait_recv()

        @pl.loop(0, n // per)
        def _(i):
            x = rows[j, pl.ds(i * per, per)].reshape(per * cap, dim)

            @pl.loop(0, ff // dim)
            def _(c):
                cols = pl.ds(pl.multiple_of(c * dim, dim), dim)
                hid[:, cols] = jnp.maximum(jnp.dot(x, up[j % 2, :, cols], preferred_element_type=f32), 0.0).astype(bf16)

            @pl.loop(0, dim // 256)
            def _(c):
                cols = pl.ds(pl.multiple_of(c * 256, 256), 256)
                y = jnp.dot(hid[...], down[j % 2, :, cols], preferred_element_type=f32).astype(bf16)
                rows[j, pl.ds(i * per, per), :, cols] = y.reshape(per, cap, 256)

        for k in order:
            send_back(j, k).start()
        own_out[j].start()
    for j in range(local):
        for k in order:
            send(j, k).wait_send()
            send_back(j, k).wait_send()
            send_back(j, k).wait_recv()
        own_out[j].wait()


def exchange(layer, n, packed, w_in, w_out):
    num_experts, cap, dim = packed.shape
    local, ff = w_in.shape[1], w_in.shape[3]
    anywhere = pl.BlockSpec(memory_space=pl.ANY)
    return pl.pallas_call(
        functools.partial(exchange_kernel, layer, n),
        in_specs=[anywhere] * 3,
        out_specs=anywhere,
        out_shape=jax.ShapeDtypeStruct(packed.shape, bf16),
        scratch_shapes=[
            pltpu.VMEM((local, n, cap, dim), bf16),
            pltpu.VMEM((2 * cap, ff), bf16),
            pltpu.VMEM((2, dim, ff), bf16),
            pltpu.VMEM((2, ff, dim), bf16),
            pltpu.SemaphoreType.DMA((2, 2)),
            pltpu.SemaphoreType.DMA((local, n)),
            pltpu.SemaphoreType.DMA((local, n)),
            pltpu.SemaphoreType.DMA((local, n)),
            pltpu.SemaphoreType.DMA((local, n)),
            pltpu.SemaphoreType.DMA((2, local)),
        ],
        compiler_params=pltpu.CompilerParams(collective_id=layer, has_side_effects=True, vmem_limit_bytes=60 * 2**20),
        cost_estimate=pl.CostEstimate(flops=4 * n * local * cap * dim * ff, bytes_accessed=4 * local * dim * ff + 8 * num_experts * cap * dim, transcendentals=0),
        name="exchange%d" % layer,
    )(packed, w_in, w_out)


def solution(mesh):
    token_spec = P(('dp', 'ep'))
    n = mesh.shape['ep']

    def per_device(x_in, pad_mask, rel_bias, expert_idx, norm_scale, w_query, w_key, w_value, w_attn_out, w_router, w_in, w_out):
        num_seqs, seq_len, model_dim = x_in.shape
        tok_count = num_seqs * seq_len
        num_layers, _, num_experts = w_router.shape
        capacity = (CAP_FACTOR * tok_count + num_experts - 1) // num_experts
        place, slot_token = routing(expert_idx.reshape(num_layers, 1, tok_count), num_experts, capacity)
        ids = expert_idx.reshape(num_layers, num_seqs, 1, seq_len)
        mask = pad_mask.reshape(num_seqs, 1, seq_len)
        router = split_router(w_router)
        hidden = x_in
        for layer in range(num_layers):
            h1, b, gate = attention(layer, num_experts, hidden, mask, rel_bias, ids, norm_scale, w_query, w_key, w_value, w_attn_out, router)
            packed = jnp.take(b.reshape(tok_count, model_dim), slot_token[layer].reshape(-1), axis=0, mode='clip')
            back = exchange(layer, n, packed.reshape(num_experts, capacity, model_dim), w_in, w_out)
            spot = place[layer, 0]
            u = jnp.take(back.reshape(-1, model_dim), jnp.maximum(spot, 0), axis=0, mode='clip').astype(f32)
            h1 = h1.reshape(tok_count, model_dim).astype(f32)
            hidden = jnp.where(spot[:, None] >= 0, h1 + gate.reshape(-1, 1) * u, h1).astype(bf16).reshape(x_in.shape)
        return hidden

    return jax.shard_map(per_device, mesh=mesh, in_specs=(token_spec, token_spec, P(), P(None, ('dp', 'ep')), P(), P(), P(), P(), P(), P(), P(None, 'ep'), P(None, 'ep')), out_specs=token_spec, check_vma=False)
```

time: 1650 us -> 969 us (0.59)
  Pallas kernels: 0 us -> 791 us
  matrix products: 474 us -> 0 us
  local copies, waits for them, and re-layouts: 518 us -> 146 us
  blocking collectives: 322 us -> 0 us
  other arithmetic: 217 us -> 22.2 us
  waiting for transfers between devices: 92.2 us -> 0 us
    pallas_call x0 -> x5, Pallas kernels: none -> 791 us  [the longest x2 619 us: exchange(): pl.pallas_call(functools.partial(exchange_kernel, layer, n), in_specs=[an...]
    dot_general x16 -> x0, matrix products: 386 us -> none  [the longest x2 106 us: expert_ffn(): jnp.einsum('ecd,edf->ecf', rows_in, up_w, preferred_element_type=jnp.floa...]
    all_to_all x2 -> x0, blocking collectives: 322 us -> none  [per_device(): received = lax.all_to_all(packed, 'ep', 0, 1, tiled=True)]
    convert_element_type x8 -> x0, local copies, waits for them, and re-layouts: 138 us -> none  [the longest x2 76.3 us: expert_ffn(): jnp.einsum('ecf,efd->ecd', inner_act, down_w, preferred_element_type=jnp....]
    gather x12 -> x4, local copies, waits for them, and re-layouts: 265 us -> 140 us  [the longest x2 91.1 us: per_device(): jnp.take(b.reshape(tok_count, model_dim), slot_token[layer].reshape(-1),...]
    all_to_all x2 -> x0, waiting for transfers between devices: 92.2 us -> none  [per_device(): returned = lax.all_to_all(expert_rows, 'ep', 1, 0, tiled=True)]
    sub x2 -> x0, matrix products: 87.3 us -> none  [attention(): attn_probs = jax.nn.softmax(scores, axis=-1).astype(jnp.bfloat16)]
    scatter x4 -> x0, local copies, waits for them, and re-layouts: 70 us -> none  [the longest x2 35.2 us: dispatch(): jnp.full((num_experts * capacity,), tok_count, jnp.int32).at[flat_slot]]
  transfers between devices with their start and end apart: 2 -> 0, of which waited for: 1 -> 0; matrix products, arithmetic and copies ran while one was open for 15% -> 0% of each run, Pallas kernels for 0% -> 0%
where the time goes in v1:
time: 969 us; the launch traced here: 960 us
  Pallas kernels  791 us (82%)
  local copies, waits for them, and re-layouts  146 us (15%)
  other arithmetic  22.2 us (2%)
    pallas_call x2, Pallas kernels, exchange(): pl.pallas_call(functools.partial(exchange_kernel, layer, n), in_specs=[an...  619 us
    pallas_call x2, Pallas kernels, attention(): pl.pallas_call(functools.partial(attention_kernel, num_experts), grid=(nu...  156 us
    gather x2, local copies, waits for them, and re-layouts, per_device(): jnp.take(b.reshape(tok_count, model_dim), slot_token[layer].reshape(-1),...  91.1 us
    gather x2, local copies, waits for them, and re-layouts, per_device(): jnp.take(back.reshape(-1, model_dim), jnp.maximum(spot, 0), axis=0, mode=...  48.7 us

profile of v1, /device:TPU:81, one launch (start us, length us, event | category | flops | bytes accessed | tf_op | source)
XLA Modules:
  0.0 960.0 jit_solution(11422791793094438126)
XLA Ops:
  0.0 0.9 reduce_precision.9
  0.9 0.3 copy.25
  1.2 1.2 copy.26
  2.4 0.2 reduce-precision_convert_fusion
  2.7 1.1 maximum_maximum_fusion.wr_ref
  3.8 1.4 copy.28.ids_ref
  5.2 1.3 reshape.106.mask_ref
  6.6 77.7 %attention.2 = (bf16[12,384,768]{2,1,0:T(8,128)(2,1)}, bf16[12,384,768]{2,1,0:T(8,128)(2,1)}, f32[12,1,384]{2,1,0:T(1,128)}) custom-call(bf16[12,384,768]{2,1,0:T(8,128)(2,1)} %x_ref.1, s32[12,1,384]{2,1,0:T(1,128)} %reshape.106.mask_ref, f32[12,384,384]{2,1,0:T(8,128)} %bias_ref.3, f32[2,2,768]{2,1,0:T(2,128)} %gain_ref.3, bf16[2,768,768]{2,1,0:T(8,128)(2,1)} %wq_ref.3, ...), custom_call_target="tpu_custom_call" | custom-call | flops 27179089920 | bytes 28311552 | tf_op jit(solution)/shard_map/attention/pallas_call | solution.py:126
  84.3 0.7 copy.24.ids_ref
  85.0 15.8 %routing.1 = (s32[2,1,4608]{2,1,0:T(1,128)}, s32[2,32,288]{2,1,0:T(8,128)}) custom-call(s32[2,1,4608]{2,1,0:T(1,128)} %copy.24.ids_ref), custom_call_target="tpu_custom_call" | custom-call | tf_op jit(solution)/shard_map/routing/pallas_call | solution.py:47
  100.7 1.4 fusion.4
  102.3 45.6 %gather_fusion = bf16[9216,768]{1,0:T(8,128)(2,1)} fusion(bf16[4608,768]{1,0:T(8,128)(2,1)} %bitcast.18, s32[9216]{0:T(1024)S(1)} %broadcast_clamp_fusion.1), kind=kCustom, calls=%fused_computation | custom fusion | bytes 28348416 | tf_op jit(solution)/shard_map/jit(_take)/gather | solution.py:265
  147.9 310.9 %exchange0.1 = bf16[32,288,768]{2,1,0:T(8,128)(2,1)} custom-call(bf16[32,288,768]{2,1,0:T(8,128)(2,1)} %bitcast.24, bf16[2,4,768,3072]{3,2,1,0:T(8,128)(2,1)} %w_in_ref.3, bf16[2,4,3072,768]{3,2,1,0:T(8,128)(2,1)} %w_out_ref.3), custom_call_target="tpu_custom_call" | custom-call | flops 86973087744 | bytes 94371840 | tf_op jit(solution)/shard_map/exchange0/pallas_call | solution.py:226
  458.8 0.1 maximum_reduce_fusion
  458.9 0.6 pad_clamp_fusion
  459.5 24.4 %gather_fusion.1 = bf16[4608,768]{1,0:T(8,128)(2,1)} fusion(bf16[9216,768]{1,0:T(8,128)(2,1)} %bitcast.20, s32[5120]{0:T(1024)S(1)} %get-tuple-element.31), kind=kCustom, calls=%fused_computation.1 | custom fusion | bytes 14174208 | tf_op jit(solution)/shard_map/jit(_take)/gather | solution.py:268
  483.9 0.7 compare_reduce_fusion.1
  484.6 9.3 fusion.x_ref
  493.8 77.8 %attention.3 = (bf16[12,384,768]{2,1,0:T(8,128)(2,1)}, bf16[12,384,768]{2,1,0:T(8,128)(2,1)}, f32[12,1,384]{2,1,0:T(1,128)}) custom-call(bf16[12,384,768]{2,1,0:T(8,128)(2,1)} %fusion.x_ref, s32[12,1,384]{2,1,0:T(1,128)} %reshape.106.mask_ref, f32[12,384,384]{2,1,0:T(8,128)} %bias_ref.3, f32[2,2,768]{2,1,0:T(2,128)} %gain_ref.3, ...), custom_call_target="tpu_custom_call" | custom-call | flops 27179089920 | bytes 28311552 | tf_op jit(solution)/shard_map/attention/pallas_call | solution.py:126
  571.7 0.1 reshape.134
  571.8 45.5 %gather_fusion.2 = bf16[9216,768]{1,0:T(8,128)(2,1)} fusion(bf16[4608,768]{1,0:T(8,128)(2,1)} %bitcast.19, s32[9216]{0:T(1024)S(1)} %broadcast_clamp_fusion), kind=kCustom, calls=%fused_computation.2 | custom fusion | bytes 28348416 | tf_op jit(solution)/shard_map/jit(_take)/gather | solution.py:265
  617.3 308.5 %exchange1.1 = bf16[32,288,768]{2,1,0:T(8,128)(2,1)} custom-call(bf16[32,288,768]{2,1,0:T(8,128)(2,1)} %bitcast.25, bf16[2,4,768,3072]{3,2,1,0:T(8,128)(2,1)} %w_in_ref.3, bf16[2,4,3072,768]{3,2,1,0:T(8,128)(2,1)} %w_out_ref.3), custom_call_target="tpu_custom_call" | custom-call | flops 86973087744 | bytes 94371840 | tf_op jit(solution)/shard_map/exchange1/pallas_call | solution.py:226
  925.9 24.4 %gather_fusion.3 = bf16[4608,768]{1,0:T(8,128)(2,1)} fusion(bf16[9216,768]{1,0:T(8,128)(2,1)} %bitcast.21, s32[5120]{0:T(1024)S(1)} %copy-done.3), kind=kCustom, calls=%fused_computation.3 | custom fusion | bytes 14174208 | tf_op jit(solution)/shard_map/jit(_take)/gather | solution.py:268
  950.3 9.3 fusion.1
  (23 shorter events, 0.3 us)
Async XLA Ops:
  6.6 77.7 %copy-start.1 = (s32[2,12,384]{2,0,1:T(2,128)S(1)}, s32[2,12,384]{2,0,1:T(2,128)}, u32[]{:S(2)}) copy-start(s32[2,12,384]{2,0,1:T(2,128)} %param.15) | copy-start | bytes 110596
  147.9 310.9 %copy-start.2 = (s32[2,1,4608]{2,1,0:T(1,128)S(1)}, s32[2,1,4608]{2,1,0:T(1,128)}, u32[]{:S(2)}) copy-start(s32[2,1,4608]{2,1,0:T(1,128)} %get-tuple-element.13) | copy-start | bytes 110596
  459.5 24.4 %copy-start.5 = (f32[12,1,384]{2,1,0:T(1,128)S(1)}, f32[12,1,384]{2,1,0:T(1,128)}, u32[]{:S(2)}) copy-start(f32[12,1,384]{2,1,0:T(1,128)} %get-tuple-element.15) | copy-start | bytes 55300
  493.8 77.9 %copy-start = (s32[1,32,288]{2,1,0:T(8,128)S(1)}, s32[1,32,288]{2,1,0:T(8,128)}, u32[]{:S(2)}) copy-start(s32[1,32,288]{2,1,0:T(8,128)} %get-tuple-element.28) | copy-start | bytes 110596
  617.3 308.5 %copy-start.3 = (s32[5120]{0:T(1024)S(1)}, s32[5120]{0:T(1024)}, u32[]{:S(2)}) copy-start(s32[5120]{0:T(1024)} %get-tuple-element.30) | copy-start | bytes 61444
  925.9 24.4 %copy-start.6 = (f32[12,1,384]{2,1,0:T(1,128)S(1)}, f32[12,1,384]{2,1,0:T(1,128)}, u32[]{:S(2)}) copy-start(f32[12,1,384]{2,1,0:T(1,128)} %get-tuple-element.19) | copy-start | bytes 55300
  925.9 24.4 %copy-start.4 = (pred[4608]{0:T(1024)(128)(4,1)S(1)}, pred[4608]{0:T(1024)(128)(4,1)}, u32[]{:S(2)}) copy-start(pred[4608]{0:T(1024)(128)(4,1)} %get-tuple-element.21) | copy-start | bytes 13828

commit v2 on v1

v2 whole, which is shorter than its diff:
```python
import functools

import jax
import jax.numpy as jnp
from jax import lax
from jax.experimental import pallas as pl
from jax.experimental.pallas import tpu as pltpu
from jax.sharding import PartitionSpec as P

NORM_EPS = 1e-6
NEG_BIG = -1e9
CAP_FACTOR = 2
LANES = 128
SUBLANES = 8
MESH = pl.DeviceIdType.MESH
f32 = jnp.float32
bf16 = jnp.bfloat16


def routing_kernel(capacity, ids_ref, place_ref, token_ref):
    num_experts = token_ref.shape[1]
    tok_count = ids_ref.shape[2]
    expert = lax.broadcasted_iota(jnp.int32, (num_experts, LANES), 0)
    upper = (lax.broadcasted_iota(jnp.int32, (LANES, LANES), 0) <= lax.broadcasted_iota(jnp.int32, (LANES, LANES), 1)).astype(bf16)
    lane = lax.broadcasted_iota(jnp.int32, (1, LANES), 1).astype(f32)
    slot_rows = lax.broadcasted_iota(jnp.int32, (capacity, LANES), 0)
    seen = jnp.zeros((num_experts, 1), f32)
    found = jnp.zeros((capacity, 2 * num_experts), f32)
    for blk in range(tok_count // LANES):
        span = slice(blk * LANES, (blk + 1) * LANES)
        ids = ids_ref[0, :, span]
        hot = jnp.where(expert == ids, 1.0, 0.0)
        count = jnp.dot(hot.astype(bf16), upper, preferred_element_type=f32) + seen
        slot = jnp.sum(hot * count, axis=0, keepdims=True).astype(jnp.int32) - 1
        seen = count[:, LANES - 1:]
        place_ref[0, :, span] = jnp.where(slot < capacity, ids * capacity + slot, -1)
        in_slot = jnp.where(slot_rows == slot, 1.0, 0.0).astype(bf16)
        names = jnp.concatenate([hot * lane, hot * blk], axis=0).astype(bf16)
        found = found + lax.dot_general(in_slot, names, (((1,), (1,)), ((), ())), preferred_element_type=f32)
    found = found.T
    token_ref[0] = (found[num_experts:] * LANES + found[:num_experts]).astype(jnp.int32)


def routing(ids, num_experts, capacity):
    layers, _, tok_count = ids.shape
    row = pl.BlockSpec((1, 1, tok_count), lambda i: (i, 0, 0))
    return pl.pallas_call(
        functools.partial(routing_kernel, capacity),
        grid=(layers,),
        in_specs=[row],
        out_specs=[row, pl.BlockSpec((1, num_experts, capacity), lambda i: (i, 0, 0))],
        out_shape=[jax.ShapeDtypeStruct((layers, 1, tok_count), jnp.int32), jax.ShapeDtypeStruct((layers, num_experts, capacity), jnp.int32)],
        name="routing",
    )(ids)


def split_router(weight):
    hi = lax.reduce_precision(weight, 8, 7)
    mid = lax.reduce_precision(weight - hi, 8, 7)
    lo = lax.reduce_precision(weight - hi - mid, 8, 7)
    pad = jnp.zeros(weight.shape[:-1] + (LANES - 3 * weight.shape[-1],), weight.dtype)
    return jnp.concatenate([hi, mid, lo, pad], axis=-1).astype(bf16)


def combined(h1, u, gate, spot):
    return jnp.where(spot >= 0, h1 + gate * u, h1).astype(bf16)


def attention_kernel(num_experts, blended, *refs):
    refs = list(refs)
    if blended:
        u_ref, past_gate_ref, spot_ref = refs[:3]
        refs = refs[3:]
    x_ref, mask_ref, bias_ref, gain_ref, wq_ref, wk_ref, wv_ref, wo_ref, wr_ref, ids_ref, h1_ref, gate_ref, tiles_ref, ctx_ref = refs
    seq_len, model_dim = x_ref.shape[1:]
    num_heads = bias_ref.shape[0]
    head_dim = ctx_ref.shape[1] // num_heads
    chunks = model_dim // LANES
    gains = gain_ref[0]
    if blended:
        lines = jnp.concatenate([past_gate_ref[0], spot_ref[0].astype(f32), jnp.zeros((6, seq_len), f32)], axis=0).T
        x = combined(x_ref[0].astype(f32), u_ref[0].astype(f32), lines[:, 0:1], lines[:, 1:2]).astype(f32)
    else:
        x = x_ref[0].astype(f32)
    a = (x * lax.rsqrt(jnp.mean(x * x, axis=-1, keepdims=True) + NORM_EPS) * gains[0:1]).astype(bf16)
    q = jnp.dot(a, wq_ref[0], preferred_element_type=f32).astype(bf16)
    k = jnp.dot(a, wk_ref[0], preferred_element_type=f32).astype(bf16)
    v = jnp.dot(a, wv_ref[0], preferred_element_type=f32).astype(bf16)
    mask_add = jnp.where(mask_ref[0] > 0, 0.0, NEG_BIG)
    first = lax.broadcasted_iota(jnp.int32, (seq_len, 2 * head_dim), 1) < head_dim
    zero = jnp.zeros((seq_len, 2 * head_dim), bf16)

    def probs(scores, head):
        scores = scores + bias_ref[head] + mask_add
        e = jnp.exp(scores - jnp.max(scores, axis=-1, keepdims=True))
        return (e * (1.0 / jnp.sum(e, axis=-1, keepdims=True))).astype(bf16)

    for pair in range(num_heads // 2):
        lanes = slice(2 * head_dim * pair, 2 * head_dim * (pair + 1))
        kp, vp = k[:, lanes], v[:, lanes]
        keys = jnp.concatenate([jnp.where(first, kp, zero), jnp.where(first, zero, kp)], axis=0)
        values = jnp.concatenate([jnp.where(first, vp, zero), jnp.where(first, zero, vp)], axis=0)
        s = lax.dot_general(q[:, lanes], keys, (((1,), (1,)), ((), ())), preferred_element_type=f32)
        p = jnp.concatenate([probs(s[:, :seq_len], 2 * pair), probs(s[:, seq_len:], 2 * pair + 1)], axis=1)
        ctx_ref[:, lanes] = jnp.dot(p, values, preferred_element_type=f32).astype(bf16)
    h1 = (x + jnp.dot(ctx_ref[...], wo_ref[0], preferred_element_type=f32)).astype(bf16)
    h1_ref[0] = h1
    h = h1.astype(f32)
    r = h * lax.rsqrt(jnp.mean(h * h, axis=-1, keepdims=True) + NORM_EPS) * gains[1:2]
    for c in range(chunks):
        tiles_ref[pl.ds(c, seq_len, stride=SUBLANES), :] = r[:, c * LANES:(c + 1) * LANES]
    b = r.astype(bf16)
    rest = r - b.astype(f32)
    mid = rest.astype(bf16)
    tail = (rest - mid.astype(f32)).astype(bf16)
    wr = wr_ref[0]
    lane = lax.broadcasted_iota(jnp.int32, (1, LANES), 1)
    part0 = jnp.dot(b, wr, preferred_element_type=f32)
    part1 = jnp.dot(mid, wr, preferred_element_type=f32)
    part2 = jnp.dot(tail, wr, preferred_element_type=f32)
    parts = part0 + jnp.where(lane < 2 * num_experts, part1, 0.0) + jnp.where(lane < num_experts, part2, 0.0)
    parts = parts.T
    logits = parts[:num_experts] + (parts[num_experts:2 * num_experts] + parts[2 * num_experts:3 * num_experts])
    e = jnp.exp(logits - jnp.max(logits, axis=0, keepdims=True))
    chosen = lax.broadcasted_iota(jnp.int32, (num_experts, seq_len), 0) == ids_ref[0, 0]
    gate_ref[0] = jnp.sum(jnp.where(chosen, e, 0.0), axis=0, keepdims=True) / jnp.sum(e, axis=0, keepdims=True)


def attention(layer, num_experts, past, x, mask, bias, ids, gains, wq, wk, wv, wo, wr):
    num_seqs, seq_len, model_dim = x.shape
    num_heads = bias.shape[0]
    inner = wq.shape[2]
    once = pl.Buffered(1)
    rows = pl.BlockSpec((1, seq_len, model_dim), lambda i: (i, 0, 0))
    line = pl.BlockSpec((1, 1, seq_len), lambda i: (i, 0, 0))

    def of_layer(array):
        return pl.BlockSpec((1,) + array.shape[1:], lambda i: (layer, 0, 0), pipeline_mode=once)

    weights = [gains, wq, wk, wv, wo, wr]
    flops = 2 * num_seqs * seq_len * (4 * model_dim * inner + 2 * seq_len * inner)
    return pl.pallas_call(
        functools.partial(attention_kernel, num_experts, bool(past)),
        grid=(num_seqs,),
        in_specs=[rows, line, line][:len(past)]
        + [rows, line, pl.BlockSpec(bias.shape, lambda i: (0, 0, 0), pipeline_mode=once)]
        + [of_layer(w) for w in weights]
        + [pl.BlockSpec((1, 1, 1, seq_len), lambda i: (layer, i, 0, 0))],
        out_specs=[rows, line, pl.BlockSpec((seq_len * SUBLANES, LANES), lambda i: (i, 0))],
        out_shape=[jax.ShapeDtypeStruct(x.shape, bf16), jax.ShapeDtypeStruct((num_seqs, 1, seq_len), f32), jax.ShapeDtypeStruct((num_seqs * seq_len * SUBLANES, LANES), f32)],
        scratch_shapes=[pltpu.VMEM((seq_len, inner), bf16)],
        compiler_params=pltpu.CompilerParams(vmem_limit_bytes=56 * 2**20),
        cost_estimate=pl.CostEstimate(flops=flops, bytes_accessed=8 * num_seqs * seq_len * model_dim, transcendentals=num_seqs * num_heads * seq_len * seq_len),
        name="attention%d" % layer,
    )(*past, x, mask, bias, *weights, ids)


def exchange_kernel(layer, n, token_ref, tiles_ref, w_in_ref, w_out_ref, out_ref, src, stage, outgoing, rows, hid, up, down, load_sem, send_sem, recv_sem, ret_send, ret_recv, own_sem):
    local, _, cap, dim = rows.shape
    ff = up.shape[1]
    per = hid.shape[0] // cap
    me = lax.axis_index("ep")
    order = sorted(range(1, n), key=lambda k: abs(k - n // 2))
    fetch = pltpu.make_async_copy(tiles_ref, src, load_sem.at[2])

    def load(j):
        return (
            pltpu.make_async_copy(w_in_ref.at[layer, j], up, load_sem.at[0]),
            pltpu.make_async_copy(w_out_ref.at[layer, j], down, load_sem.at[1]),
        )

    def send(j, k):
        peer = lax.rem(me + k, n)
        return pltpu.make_async_remote_copy(
            src_ref=outgoing.at[j % 2, k],
            dst_ref=rows.at[j, me],
            send_sem=send_sem.at[j, k],
            recv_sem=recv_sem.at[j, k],
            device_id={"ep": peer},
            device_id_type=MESH,
        )

    def send_back(j, k):
        peer = lax.rem(me + k, n)
        return pltpu.make_async_remote_copy(
            src_ref=rows.at[j, peer],
            dst_ref=out_ref.at[me * local + j],
            send_sem=ret_send.at[j, k],
            recv_sem=ret_recv.at[j, k],
            device_id={"ep": peer},
            device_id_type=MESH,
        )

    def gather(j, k, dst):
        base = (lax.rem(me + k, n) * local + j) * cap

        @pl.loop(0, cap // 16)
        def _(i):
            for sub in range(16):
                stage[pl.ds(pl.multiple_of((i * 16 + sub) * SUBLANES, SUBLANES), SUBLANES), :] = src[token_ref[base + i * 16 + sub]]

        for c in range(dim // LANES):
            dst[:, c * LANES:(c + 1) * LANES] = stage[pl.ds(c, cap, stride=SUBLANES), :].astype(bf16)

    def kth(m):
        half = (m + 1) // 2
        return n // 2 + jnp.where(m % 2 == 0, half, -half)

    def dispatch(j):
        if j >= 2:
            for k in order:
                send(j - 2, k).wait_send()
        gather(j, n // 2, outgoing.at[j % 2, n // 2])

        @pl.loop(1, n - 1)
        def _(m):
            gather(j, kth(m), outgoing.at[j % 2, kth(m)])
            send(j, kth(m - 1)).start()

        gather(j, 0, rows.at[j, me])
        send(j, order[-1]).start()

    def expert(j):
        for k in order:
            send(j, k).wait_recv()
        for c in load(j):
            c.wait()

        @pl.loop(0, n // per)
        def _(i):
            x = rows[j, pl.ds(i * per, per)].reshape(per * cap, dim)

            @pl.loop(0, ff // dim)
            def _(c):
                cols = pl.ds(pl.multiple_of(c * dim, dim), dim)
                hid[:, cols] = jnp.maximum(jnp.dot(x, up[:, cols], preferred_element_type=f32), 0.0).astype(bf16)

            @pl.loop(0, dim // 256)
            def _(c):
                cols = pl.ds(pl.multiple_of(c * 256, 256), 256)
                y = jnp.dot(hid[...], down[:, cols], preferred_element_type=f32).astype(bf16)
                rows[j, pl.ds(i * per, per), :, cols] = y.reshape(per, cap, 256)

        if j + 1 < local:
            for c in load(j + 1):
                c.start()
        for k in order:
            send_back(j, k).start()
        own_out[j].start()

    own_out = [pltpu.make_async_copy(rows.at[j, me], out_ref.at[me * local + j], own_sem.at[j]) for j in range(local)]
    fetch.start()
    barrier = pltpu.get_barrier_semaphore()
    for k in range(1, n):
        pl.semaphore_signal(barrier, inc=1, device_id={"ep": lax.rem(me + k, n)}, device_id_type=MESH)
    pl.semaphore_wait(barrier, n - 1)
    fetch.wait()
    for c in load(0):
        c.start()
    for j in range(local):
        dispatch(j)
        if j >= 2:
            expert(j - 2)
    for j in range(max(local - 2, 0), local):
        expert(j)
    for j in range(local):
        for k in order:
            if j >= local - 2:
                send(j, k).wait_send()
            send_back(j, k).wait_send()
            send_back(j, k).wait_recv()
        own_out[j].wait()


def exchange(layer, n, slot_token, tiles, w_in, w_out):
    num_experts, cap = slot_token.shape
    local, dim, ff = w_in.shape[1:]
    anywhere = pl.BlockSpec(memory_space=pl.ANY)
    dma = pltpu.SemaphoreType.DMA
    return pl.pallas_call(
        functools.partial(exchange_kernel, layer, n),
        in_specs=[pl.BlockSpec(memory_space=pltpu.SMEM)] + [anywhere] * 3,
        out_specs=anywhere,
        out_shape=jax.ShapeDtypeStruct((num_experts, cap, dim), bf16),
        scratch_shapes=[
            pltpu.VMEM((tiles.shape[0] // SUBLANES, SUBLANES, LANES), f32),
            pltpu.VMEM((cap * SUBLANES, LANES), f32),
            pltpu.VMEM((2, n, cap, dim), bf16),
            pltpu.VMEM((local, n, cap, dim), bf16),
            pltpu.VMEM((2 * cap, ff), bf16),
            pltpu.VMEM((dim, ff), bf16),
            pltpu.VMEM((ff, dim), bf16),
            dma((3,)),
            dma((local, n)),
            dma((local, n)),
            dma((local, n)),
            dma((local, n)),
            dma((local,)),
        ],
        compiler_params=pltpu.CompilerParams(collective_id=layer, has_side_effects=True, vmem_limit_bytes=62 * 2**20),
        cost_estimate=pl.CostEstimate(flops=4 * n * local * cap * dim * ff, bytes_accessed=4 * local * dim * ff + 8 * num_experts * cap * dim, transcendentals=0),
        name="exchange%d" % layer,
    )(slot_token.reshape(-1), tiles.reshape(-1, SUBLANES, LANES), w_in, w_out)


def solution(mesh):
    token_spec = P(('dp', 'ep'))
    n = mesh.shape['ep']

    def per_device(x_in, pad_mask, rel_bias, expert_idx, norm_scale, w_query, w_key, w_value, w_attn_out, w_router, w_in, w_out):
        num_seqs, seq_len, model_dim = x_in.shape
        tok_count = num_seqs * seq_len
        num_layers, _, num_experts = w_router.shape
        capacity = (CAP_FACTOR * tok_count + num_experts - 1) // num_experts
        place, slot_token = routing(expert_idx.reshape(num_layers, 1, tok_count), num_experts, capacity)
        ids = expert_idx.reshape(num_layers, num_seqs, 1, seq_len)
        mask = pad_mask.reshape(num_seqs, 1, seq_len)
        router = split_router(w_router)
        hidden, past = x_in, ()
        for layer in range(num_layers):
            h1, gate, tiles = attention(layer, num_experts, past, hidden, mask, rel_bias, ids, norm_scale, w_query, w_key, w_value, w_attn_out, router)
            back = exchange(layer, n, slot_token[layer], tiles, w_in, w_out)
            spot = place[layer, 0]
            u = jnp.take(back.reshape(-1, model_dim), jnp.maximum(spot, 0), axis=0, mode='clip')
            hidden, past = h1, (u.reshape(x_in.shape), gate, spot.reshape(num_seqs, 1, seq_len))
        shape = (num_seqs, seq_len, 1)
        return combined(h1.astype(f32), past[0].astype(f32), gate.reshape(shape), spot.reshape(shape))

    return jax.shard_map(per_device, mesh=mesh, in_specs=(token_spec, token_spec, P(), P(None, ('dp', 'ep')), P(), P(), P(), P(), P(), P(), P(None, 'ep'), P(None, 'ep')), out_specs=token_spec, check_vma=False)
```

time: 969 us -> 883 us (0.911)
  local copies, waits for them, and re-layouts: 146 us -> 56 us
  Pallas kernels: 791 us -> 806 us
  other arithmetic: 22.2 us -> 12.2 us
    gather x2 -> x0, local copies, waits for them, and re-layouts: 91.1 us -> none  [per_device(): jnp.take(b.reshape(tok_count, model_dim), slot_token[layer].reshape(-1),...]
    pallas_call x4, Pallas kernels: 775 us -> 797 us  [the longest x2 633 us: exchange(): pl.pallas_call(functools.partial(exchange_kernel, layer, n), in_specs=[pl...]
where the time goes in v2:
time: 883 us; the launch traced here: 874 us
  Pallas kernels  806 us (91%)
  local copies, waits for them, and re-layouts  56 us (6%)
  other arithmetic  12.2 us (1%)
    pallas_call x2, Pallas kernels, exchange(): pl.pallas_call(functools.partial(exchange_kernel, layer, n), in_specs=[pl...  633 us
    pallas_call x2, Pallas kernels, attention(): pl.pallas_call(functools.partial(attention_kernel, num_experts, bool(past...  164 us
    gather x2, local copies, waits for them, and re-layouts, per_device(): jnp.take(back.reshape(-1, model_dim), jnp.maximum(spot, 0), axis=0, mode=...  48.7 us

profile of v2, /device:TPU:81, one launch (start us, length us, event | category | flops | bytes accessed | tf_op | source)
XLA Modules:
  0.0 874.5 jit_solution(7153611485330249167)
XLA Ops:
  0.0 1.5 copy.24.ids_ref
  1.5 9.1 %routing.1 = (s32[2,1,4608]{2,1,0:T(1,128)}, s32[2,32,288]{2,1,0:T(8,128)}) custom-call(s32[2,1,4608]{2,1,0:T(1,128)} %copy.24.ids_ref), custom_call_target="tpu_custom_call" | custom-call | tf_op jit(solution)/shard_map/routing/pallas_call | solution.py:47
  10.6 0.8 fusion.3
  11.4 0.7 reshape_squeeze.12.token_ref
  12.1 0.7 reshape_squeeze.10.token_ref
  12.8 1.3 reshape.63.refs_1_.refs_4_
  14.1 1.2 copy.26
  15.3 0.9 reduce_precision.9
  16.3 0.3 copy.25
  16.5 0.2 reduce-precision_convert_fusion
  16.8 0.1 pad.3.clone
  16.8 1.1 maximum_maximum_fusion.refs_8_.refs_11_
  18.0 0.7 copy.28.refs_9_.refs_12_
  18.6 78.4 %attention0.1 = (bf16[12,384,768]{2,1,0:T(8,128)(2,1)}, f32[12,1,384]{2,1,0:T(1,128)}, f32[36864,128]{1,0:T(8,128)}) custom-call(bf16[12,384,768]{2,1,0:T(8,128)(2,1)} %refs_0_.1, s32[12,1,384]{2,1,0:T(1,128)} %reshape.63.refs_1_.refs_4_, f32[12,384,384]{2,1,0:T(8,128)} %refs_5_.3, f32[2,2,768]{2,1,0:T(2,128)} %refs_6_.3, bf16[2,768,768]{2,1,0:T(8,128)(2,1)} %refs_7_.3, ...), custom_call_target="tpu_custom_call" | custom-call | flops 27179089920 | bytes 28311552 | tf_op jit(solution)/shard_map/attention0/pallas_call | solution.py:142
  97.0 317.5 %exchange0.1 = bf16[32,288,768]{2,1,0:T(8,128)(2,1)} custom-call(s32[9216]{0:T(1024)} %reshape_squeeze.10.token_ref, f32[4608,8,128]{2,1,0:T(8,128)} %bitcast.22, bf16[2,4,768,3072]{3,2,1,0:T(8,128)(2,1)} %w_in_ref.3, bf16[2,4,3072,768]{3,2,1,0:T(8,128)(2,1)} %w_out_ref.3), custom_call_target="tpu_custom_call" | custom-call | flops 86973087744 | bytes 94371840 | tf_op jit(solution)/shard_map/exchange0/pallas_call | solution.py:280
  414.6 0.0 copy-done.1
  414.6 0.7 maximum_reduce_fusion
  415.2 24.4 %gather_fusion = bf16[4608,768]{1,0:T(8,128)(2,1)} fusion(bf16[9216,768]{1,0:T(8,128)(2,1)} %bitcast.13, s32[5120]{0:T(1024)S(1)} %get-tuple-element.30), kind=kCustom, calls=%fused_computation | custom fusion | bytes 14174208 | tf_op jit(solution)/shard_map/jit(_take)/gather | solution.py:324
  439.6 85.6 %attention1.1 = (bf16[12,384,768]{2,1,0:T(8,128)(2,1)}, f32[12,1,384]{2,1,0:T(1,128)}, f32[36864,128]{1,0:T(8,128)}) custom-call(bf16[12,384,768]{2,1,0:T(8,128)(2,1)} %bitcast.16, f32[12,1,384]{2,1,0:T(1,128)} %get-tuple-element.16.refs_1_, s32[12,1,384]{2,1,0:T(1,128)} %bitcast.20, bf16[12,384,768]{2,1,0:T(8,128)(2,1)} %get-tuple-element.17.refs_3_, ...), custom_call_target="tpu_custom_call" | custom-call | flops 27179089920 | bytes 28311552 | tf_op jit(solution)/shard_map/attention1/pallas_call | solution.py:142
  525.2 315.1 %exchange1.1 = bf16[32,288,768]{2,1,0:T(8,128)(2,1)} custom-call(s32[9216]{0:T(1024)} %reshape_squeeze.12.token_ref, f32[4608,8,128]{2,1,0:T(8,128)} %bitcast.21, bf16[2,4,768,3072]{3,2,1,0:T(8,128)(2,1)} %w_in_ref.3, bf16[2,4,3072,768]{3,2,1,0:T(8,128)(2,1)} %w_out_ref.3), custom_call_target="tpu_custom_call" | custom-call | flops 86973087744 | bytes 94371840 | tf_op jit(solution)/shard_map/exchange1/pallas_call | solution.py:280
  840.3 24.4 %gather_fusion.1 = bf16[4608,768]{1,0:T(8,128)(2,1)} fusion(bf16[9216,768]{1,0:T(8,128)(2,1)} %bitcast.14, s32[5120]{0:T(1024)S(1)} %get-tuple-element.29), kind=kCustom, calls=%fused_computation.1 | custom fusion | bytes 14174208 | tf_op jit(solution)/shard_map/jit(_take)/gather | solution.py:324
  864.7 0.0 copy-done.2
  864.7 0.1 compare_reduce_fusion
  864.8 9.3 %fusion = bf16[12,384,768]{2,1,0:T(8,128)(2,1)} fusion(bf16[12,384,768]{2,1,0:T(8,128)(2,1)} %bitcast.15, bf16[12,384,768]{2,1,0:T(8,128)(2,1)} %get-tuple-element.18, f32[12,384]{1,0:T(8,128)S(1)} %bitcast.19, pred[12,384]{1,0:T(8,128)(4,1)S(1)} %ge.16), kind=kLoop, calls=%fused_computation.3 | loop fusion | flops 21233664 | bytes 21256704 | tf_op jit(solution)/shard_map/convert_element_type | solution.py:66
  (10 shorter events, 0.0 us)
Async XLA Ops:
  0.0 18.0 %copy-start = (s32[2,12,384]{2,0,1:T(2,128)S(1)}, s32[2,12,384]{2,0,1:T(2,128)}, u32[]{:S(2)}) copy-start(s32[2,12,384]{2,0,1:T(2,128)} %param.15) | copy-start | bytes 110596
  97.0 317.6 %copy-start.1 = (s32[2,1,4608]{2,1,0:T(1,128)S(1)}, s32[2,1,4608]{2,1,0:T(1,128)}, u32[]{:S(2)}) copy-start(s32[2,1,4608]{2,1,0:T(1,128)} %get-tuple-element.13) | copy-start | bytes 110596
  840.3 24.4 %copy-start.3 = (f32[12,1,384]{2,1,0:T(1,128)S(1)}, f32[12,1,384]{2,1,0:T(1,128)}, u32[]{:S(2)}) copy-start(f32[12,1,384]{2,1,0:T(1,128)} %get-tuple-element.19) | copy-start | bytes 55300
  840.3 24.4 %copy-start.2 = (s32[2,1,4608]{2,1,0:T(1,128)S(1)}, s32[2,1,4608]{2,1,0:T(1,128)}, u32[]{:S(2)}) copy-start(s32[2,1,4608]{2,1,0:T(1,128)} %get-tuple-element.13) | copy-start | bytes 110596
